TPU v7x, 32 devices: a whole 2x2x4 slice. The times are simulated.
32 devices in a mesh: prow: 8 (over z, x), pcol: 4 (over y, core).
Axes of the slice: x: 2, y: 2, z: 4, core: 2. Of those that a mesh axis runs over, the one named last changes fastest.
Arguments:
- matrix: float32 [16384, 16384], P('prow', 'pcol'), may hold values from -6 to 6
Outputs:
- reduced: float32 [16384, 16384], P('prow', 'pcol')
- householder_coefficients: float32 [2, 8], replicated
All inputs are finite; a program needn't handle non-finite values.
Results may differ from a plain program's by a relative error of at most 0.0003.
Values sent between devices are 32-bit elements; how exact they have to be, the bound alone decides.
No kernel may reach another device: no remote copies, remote signals or barrier semaphores. Data moves between devices by JAX's collectives and lax.ppermute only.
A program may use at most 128 MiB of HBM per device.

v0:
```python
import jax
import jax.numpy as jnp
from jax import lax
from jax.sharding import PartitionSpec as P

NB = 8
epsilon = 1e-06


def from_root(x, axis, root):
    mine = lax.axis_index(axis) == root
    return lax.psum(jnp.where(mine, x, jnp.zeros_like(x)), axis)


def precise_dot(left, right):
    return jnp.dot(left, right, precision=lax.Precision.HIGHEST)


def inner_rows(left, right):
    return lax.dot_general(left, right, (((1,), (1,)), ((), ())), precision=lax.Precision.HIGHEST)


def householder(alpha_value, sumsq):
    norm_value = jnp.sqrt(sumsq + epsilon)
    signum = jnp.where(alpha_value >= 0.0, 1.0, -1.0).astype(jnp.float32)
    beta_value = -signum * norm_value
    return (beta_value, (beta_value - alpha_value) / beta_value, alpha_value - beta_value)


def per_device(matrix):
    rows_dev, cols_dev = matrix.shape
    prow_id = lax.axis_index("prow")
    pcol_id = lax.axis_index("pcol")
    row_glob = prow_id * rows_dev + jnp.arange(rows_dev, dtype=jnp.int32)
    col_glob = pcol_id * cols_dev + jnp.arange(cols_dev, dtype=jnp.int32)
    panel_index = jnp.arange(NB, dtype=jnp.int32)
    wide_index = jnp.arange(NB + 1, dtype=jnp.int32)
    held_tile = matrix
    source_side_factor_list = []
    target_side_factor_list = []
    column_owner_rank = 0 // cols_dev
    column_local_index = 0 - column_owner_rank * cols_dev
    row_root = 0 // rows_dev
    row_local = 0 - row_root * rows_dev
    col_panel = from_root(
        held_tile[:, column_local_index : column_local_index + NB + 1].T, "pcol", column_owner_rank
    )
    row_panel = from_root(held_tile[row_local : row_local + NB, :], "prow", row_root)
    sel_rows = (row_glob[None, :] == 0 + panel_index[:, None]).astype(jnp.float32)
    sel_cols = (col_glob[None, :] == 0 + wide_index[:, None]).astype(jnp.float32)
    v_rows = jnp.zeros((NB, rows_dev), jnp.float32)
    x_rows = jnp.zeros((NB, rows_dev), jnp.float32)
    y_cols = jnp.zeros((NB, cols_dev), jnp.float32)
    u_cols = jnp.zeros((NB, cols_dev), jnp.float32)
    v_panel = jnp.zeros((NB, NB), jnp.float32)
    y_panel = jnp.zeros((NB, NB + 1), jnp.float32)
    u_panel = jnp.zeros((NB, NB + 1), jnp.float32)
    diagonal_entries = []
    super_list = []
    for i in range(NB):
        column = (
            col_panel[i] - precise_dot(y_panel[:, i], v_rows) - precise_dot(u_panel[:, i], x_rows)
        )
        masked = jnp.where(row_glob >= i, column, 0.0)
        trans_part, v_coef, x_coef, col_window, col_sumsq, x_panel = lax.psum(
            (
                precise_dot(masked, held_tile),
                precise_dot(v_rows, masked),
                precise_dot(x_rows, masked),
                precise_dot(sel_rows, masked),
                jnp.sum(masked * masked),
                inner_rows(x_rows, sel_rows),
            ),
            "prow",
        )
        row_raw = row_panel[i]
        beta_left, source_side_coefficient, denom_left = householder(col_window[i], col_sumsq)
        row_eff = row_raw - precise_dot(v_panel[:, i], y_cols) - precise_dot(x_panel[:, i], u_cols)
        transposed = (
            trans_part
            - precise_dot(v_coef, y_cols)
            - precise_dot(x_coef, u_cols)
            - beta_left * row_eff
        ) / denom_left
        y_new = jnp.where(col_glob > i, source_side_coefficient * transposed, 0.0)
        v_new = (masked - beta_left * (row_glob == i).astype(jnp.float32)) / denom_left
        v_panel = v_panel.at[i].set(
            (col_window - beta_left * (panel_index == i).astype(jnp.float32)) / denom_left
        )
        v_rows = v_rows.at[i].set(v_new)
        y_cols = y_cols.at[i].set(y_new)
        row_new = row_eff - y_new
        row_masked = jnp.where(col_glob >= i + 1, row_new, 0.0)
        prod_part, y_coef, u_coef, row_window, row_sumsq, y_panel = lax.psum(
            (
                precise_dot(held_tile, row_masked),
                precise_dot(y_cols, row_masked),
                precise_dot(u_cols, row_masked),
                precise_dot(sel_cols, row_masked),
                jnp.sum(row_masked * row_masked),
                inner_rows(y_cols, sel_cols),
            ),
            "pcol",
        )
        right_reflector_beta, target_side_coefficient, denom_right = householder(
            row_window[i + 1], row_sumsq
        )
        column_next = (
            col_panel[i + 1]
            - precise_dot(y_panel[:, i + 1], v_rows)
            - precise_dot(u_panel[:, i + 1], x_rows)
        )
        product = (
            prod_part
            - precise_dot(y_coef, v_rows)
            - precise_dot(u_coef, x_rows)
            - right_reflector_beta * column_next
        ) / denom_right
        x_new = jnp.where(row_glob > i, target_side_coefficient * product, 0.0)
        u_new = (
            row_masked - right_reflector_beta * (col_glob == i + 1).astype(jnp.float32)
        ) / denom_right
        u_panel = u_panel.at[i].set(
            (row_window - right_reflector_beta * (wide_index == i + 1).astype(jnp.float32))
            / denom_right
        )
        x_rows = x_rows.at[i].set(x_new)
        u_cols = u_cols.at[i].set(u_new)
        diagonal_entries.append(beta_left)
        super_list.append(right_reflector_beta)
        source_side_factor_list.append(source_side_coefficient)
        target_side_factor_list.append(target_side_coefficient)
    stack_left = jnp.concatenate([v_rows, x_rows], axis=0)
    stack_right = jnp.concatenate([y_cols, u_cols], axis=0)
    updated = held_tile - lax.dot_general(
        stack_left, stack_right, (((0,), (0,)), ((), ())), precision=lax.Precision.HIGHEST
    )
    col_slice = updated[:, column_local_index : column_local_index + NB]
    col_keep = jnp.logical_and(pcol_id == column_owner_rank, row_glob >= NB)[:, None]
    updated = updated.at[:, column_local_index : column_local_index + NB].set(
        jnp.where(col_keep, v_rows.T, col_slice)
    )
    row_slice = updated[row_local : row_local + NB, :]
    panel_rows_glob = (0 + panel_index)[:, None]
    col_g = col_glob[None, :]
    v_window = jnp.where(panel_index[None, :] < panel_index[:, None], v_panel.T, 0.0)
    v_part = precise_dot(v_window, sel_cols[:NB])
    diag_arr = jnp.stack(diagonal_entries)[:, None]
    super_arr = jnp.stack(super_list)[:, None]
    panel_values = jnp.where(
        col_g < 0,
        row_slice,
        jnp.where(
            col_g < panel_rows_glob,
            v_part,
            jnp.where(
                col_g == panel_rows_glob,
                diag_arr,
                jnp.where(col_g == panel_rows_glob + 1, super_arr, u_cols),
            ),
        ),
    )
    row_final = jnp.where(prow_id == row_root, panel_values, row_slice)
    held_tile = updated.at[row_local : row_local + NB, :].set(row_final)
    householder_coefficients = jnp.stack(
        [jnp.stack(source_side_factor_list), jnp.stack(target_side_factor_list)]
    )
    return (held_tile, householder_coefficients)


def solution(mesh):
    in_specs = (P("prow", "pcol"),)
    out_specs = (P("prow", "pcol"), P())
    return jax.shard_map(
        per_device, mesh=mesh, in_specs=in_specs, out_specs=out_specs, check_vma=False
    )
```

profile of v0, /device:TPU:0, one launch (start us, length us, event | category | flops | bytes accessed | tf_op | source)
XLA Modules:
  0.0 1049.0 jit_solution(7705097731152169826)
XLA Ops:
  7.2 2.3 select_bitcast_fusion
  14.8 35.1 %all-reduce.25.cloned.1.call-done = f32[9,2048]{0,1:T(8,128)} async-done(((f32[9,2048]{0,1:T(8,128)}), f32[9,2048]{0,1:T(8,128)}) %all-reduce.25.cloned.1.call-update) | async-done | bytes 73744 | tf_op jit(solution)/shard_map/psum | solution.py:12
  49.9 10.3 slice_reduce_fusion
  60.9 19.6 %fusion.321 = f32[1,4096]{1,0:T(1,128)S(1)} fusion(f32[2048,1]{0,1:T(1,128)S(1)} %bitcast.809, f32[2048,4096]{1,0:T(8,128)} %param.99), kind=kOutput, calls=%fused_computation.530 | convolution fusion | flops 100663296 | bytes 33579008 | tf_op jit(solution)/shard_map/dot_general | solution.py:16
  80.7 38.6 %all-reduce.13 = (f32[8]{0:T(128)S(1)}, f32[4096]{0:T(1024)S(1)}, f32[8]{0:T(128)S(1)}, f32[]{:T(128)}, f32[8,8]{1,0:T(8,128)S(1)}) all-reduce(f32[8]{0:T(128)S(1)} %convolution_bitcast_fusion.45, f32[4096]{0:T(1024)S(1)} %bitcast.818, f32[8]{0:T(128)S(1)} %convolution_bitcast_fusion.46, ...), channel_id=1, replica_groups=mesh['prow'=8,'pcol'=4] {'prow'}, use_global_device_ids=true, to_apply=%region_5.6 | all-reduce | flops 4177 | bytes 33416 | tf_op jit(solution)/shard_map/psum | solution.py:65
  121.5 2.9 all-reduce.27.cloned.1.call-done
  124.3 1.6 fusion.317
  127.5 30.7 %fusion.322 = f32[1,2048]{1,0:T(1,128)S(1)} fusion(f32[4096,1]{0,1:T(1,128)S(1)} %bitcast.802, f32[2048,4096]{1,0:T(8,128)} %param.99), kind=kOutput, calls=%fused_computation.531 | convolution fusion | flops 100663296 | bytes 33579008 | tf_op jit(solution)/shard_map/dot_general | solution.py:16
  158.6 11.4 %all-reduce.21 = (f32[9]{0:T(128)S(1)}, f32[]{:T(128)}, f32[8,9]{1,0:T(8,128)S(1)}, f32[8]{0:T(128)S(1)}, f32[2048]{0:T(1024)S(1)}, /*index=5*/f32[8]{0:T(128)S(1)}) all-reduce(f32[9]{0:T(128)S(1)} %convolution_bitcast_fusion.44, f32[]{:T(128)} %get-tuple-element.757, ...), channel_id=1, replica_groups=mesh['prow'=8,'pcol'=4] {'pcol'}, use_global_device_ids=true, to_apply=%region_9.10 | all-reduce | flops 2146 | bytes 17168 | tf_op jit(solution)/shard_map/psum | solution.py:94
  177.3 19.5 %fusion.323 = f32[1,4096]{1,0:T(1,128)S(1)} fusion(f32[2048,1]{0,1:T(1,128)S(1)} %bitcast.805, f32[2048,4096]{1,0:T(8,128)} %param.99), kind=kOutput, calls=%fused_computation.532 | convolution fusion | flops 100663296 | bytes 33579008 | tf_op jit(solution)/shard_map/dot_general | solution.py:16
  197.5 36.5 %all-reduce.12 = (f32[8]{0:T(128)S(1)}, f32[4096]{0:T(1024)S(1)}, f32[8]{0:T(128)S(1)}, f32[8]{0:T(128)S(1)}, f32[]{:T(128)}, /*index=5*/f32[8,8]{1,0:T(8,128)S(1)}) all-reduce(f32[8]{0:T(128)S(1)} %convolution_bitcast_fusion.40, f32[4096]{0:T(1024)S(1)} %bitcast.813, ...), channel_id=1, replica_groups=mesh['prow'=8,'pcol'=4] {'prow'}, use_global_device_ids=true, to_apply=%region_20.21 | all-reduce | flops 4185 | bytes 33480 | tf_op jit(solution)/shard_map/psum | solution.py:65
  240.9 30.7 %fusion.324 = f32[1,2048]{1,0:T(1,128)S(1)} fusion(f32[4096,1]{0,1:T(1,128)S(1)} %bitcast.774, f32[2048,4096]{1,0:T(8,128)} %param.99), kind=kOutput, calls=%fused_computation.533 | convolution fusion | flops 100663296 | bytes 33579008 | tf_op jit(solution)/shard_map/dot_general | solution.py:16
  272.0 11.2 %all-reduce.20 = (f32[9]{0:T(128)S(1)}, f32[]{:T(128)}, f32[8,9]{1,0:T(8,128)S(1)}, f32[8]{0:T(128)S(1)}, f32[2048]{0:T(1024)S(1)}, /*index=5*/f32[8]{0:T(128)S(1)}) all-reduce(f32[9]{0:T(128)S(1)} %convolution_bitcast_fusion.39, f32[]{:T(128)} %get-tuple-element.750, ...), channel_id=1, replica_groups=mesh['prow'=8,'pcol'=4] {'pcol'}, use_global_device_ids=true, to_apply=%region_23.24 | all-reduce | flops 2146 | bytes 17168 | tf_op jit(solution)/shard_map/psum | solution.py:94
  287.5 4.7 scatter.170
  296.4 19.5 %fusion.325 = f32[1,4096]{1,0:T(1,128)S(1)} fusion(f32[2048,1]{0,1:T(1,128)S(1)} %bitcast.777, f32[2048,4096]{1,0:T(8,128)} %param.99), kind=kOutput, calls=%fused_computation.534 | convolution fusion | flops 100663296 | bytes 33579008 | tf_op jit(solution)/shard_map/dot_general | solution.py:16
  316.6 34.1 %all-reduce.11 = (f32[8]{0:T(128)S(1)}, f32[4096]{0:T(1024)S(1)}, f32[8]{0:T(128)S(1)}, f32[8]{0:T(128)S(1)}, f32[]{:T(128)}, /*index=5*/f32[8,8]{1,0:T(8,128)S(1)}) all-reduce(f32[8]{0:T(128)S(1)} %convolution_bitcast_fusion.35, f32[4096]{0:T(1024)S(1)} %bitcast.811, ...), channel_id=1, replica_groups=mesh['prow'=8,'pcol'=4] {'prow'}, use_global_device_ids=true, to_apply=%region_34.35 | all-reduce | flops 4185 | bytes 33480 | tf_op jit(solution)/shard_map/psum | solution.py:65
  358.3 30.7 %fusion.326 = f32[1,2048]{1,0:T(1,128)S(1)} fusion(f32[4096,1]{0,1:T(1,128)S(1)} %bitcast.754, f32[2048,4096]{1,0:T(8,128)} %param.99), kind=kOutput, calls=%fused_computation.535 | convolution fusion | flops 100663296 | bytes 33579008 | tf_op jit(solution)/shard_map/dot_general | solution.py:16
  389.3 11.2 %all-reduce.19 = (f32[9]{0:T(128)S(1)}, f32[]{:T(128)}, f32[8,9]{1,0:T(8,128)S(1)}, f32[8]{0:T(128)S(1)}, f32[2048]{0:T(1024)S(1)}, /*index=5*/f32[8]{0:T(128)S(1)}) all-reduce(f32[9]{0:T(128)S(1)} %convolution_bitcast_fusion.34, f32[]{:T(128)} %get-tuple-element.743, ...), channel_id=1, replica_groups=mesh['prow'=8,'pcol'=4] {'pcol'}, use_global_device_ids=true, to_apply=%region_37.38 | all-reduce | flops 2146 | bytes 17168 | tf_op jit(solution)/shard_map/psum | solution.py:94
  404.4 4.7 scatter.180
  413.6 19.5 %fusion.327 = f32[1,4096]{1,0:T(1,128)S(1)} fusion(f32[2048,1]{0,1:T(1,128)S(1)} %bitcast.785, f32[2048,4096]{1,0:T(8,128)} %param.99), kind=kOutput, calls=%fused_computation.536 | convolution fusion | flops 100663296 | bytes 33579008 | tf_op jit(solution)/shard_map/dot_general | solution.py:16
  433.8 34.1 %all-reduce.10 = (f32[8]{0:T(128)S(1)}, f32[4096]{0:T(1024)S(1)}, f32[8]{0:T(128)S(1)}, f32[8]{0:T(128)S(1)}, f32[]{:T(128)}, /*index=5*/f32[8,8]{1,0:T(8,128)S(1)}) all-reduce(f32[8]{0:T(128)S(1)} %convolution_bitcast_fusion.30, f32[4096]{0:T(1024)S(1)} %bitcast.814, ...), channel_id=1, replica_groups=mesh['prow'=8,'pcol'=4] {'prow'}, use_global_device_ids=true, to_apply=%region_48.49 | all-reduce | flops 4185 | bytes 33480 | tf_op jit(solution)/shard_map/psum | solution.py:65
  475.6 30.7 %fusion.328 = f32[1,2048]{1,0:T(1,128)S(1)} fusion(f32[4096,1]{0,1:T(1,128)S(1)} %bitcast.758, f32[2048,4096]{1,0:T(8,128)} %param.99), kind=kOutput, calls=%fused_computation.537 | convolution fusion | flops 100663296 | bytes 33579008 | tf_op jit(solution)/shard_map/dot_general | solution.py:16
  506.6 11.2 %all-reduce.18 = (f32[9]{0:T(128)S(1)}, f32[]{:T(128)}, f32[8,9]{1,0:T(8,128)S(1)}, f32[8]{0:T(128)S(1)}, f32[2048]{0:T(1024)S(1)}, /*index=5*/f32[8]{0:T(128)S(1)}) all-reduce(f32[9]{0:T(128)S(1)} %convolution_bitcast_fusion.29, f32[]{:T(128)} %get-tuple-element.736, ...), channel_id=1, replica_groups=mesh['prow'=8,'pcol'=4] {'pcol'}, use_global_device_ids=true, to_apply=%region_51.52 | all-reduce | flops 2146 | bytes 17168 | tf_op jit(solution)/shard_map/psum | solution.py:94
  521.6 4.7 scatter.190
  530.8 19.5 %fusion.329 = f32[1,4096]{1,0:T(1,128)S(1)} fusion(f32[2048,1]{0,1:T(1,128)S(1)} %bitcast.789, f32[2048,4096]{1,0:T(8,128)} %param.99), kind=kOutput, calls=%fused_computation.538 | convolution fusion | flops 100663296 | bytes 33579008 | tf_op jit(solution)/shard_map/dot_general | solution.py:16
  550.9 34.1 %all-reduce.9 = (f32[8]{0:T(128)S(1)}, f32[4096]{0:T(1024)S(1)}, f32[8]{0:T(128)S(1)}, f32[8]{0:T(128)S(1)}, f32[]{:T(128)}, /*index=5*/f32[8,8]{1,0:T(8,128)S(1)}) all-reduce(f32[8]{0:T(128)S(1)} %convolution_bitcast_fusion.25, f32[4096]{0:T(1024)S(1)} %bitcast.815, ...), channel_id=1, replica_groups=mesh['prow'=8,'pcol'=4] {'prow'}, use_global_device_ids=true, to_apply=%region_62.63 | all-reduce | flops 4185 | bytes 33480 | tf_op jit(solution)/shard_map/psum | solution.py:65
  592.4 30.7 %fusion.330 = f32[1,2048]{1,0:T(1,128)S(1)} fusion(f32[4096,1]{0,1:T(1,128)S(1)} %bitcast.762, f32[2048,4096]{1,0:T(8,128)} %param.99), kind=kOutput, calls=%fused_computation.539 | convolution fusion | flops 100663296 | bytes 33579008 | tf_op jit(solution)/shard_map/dot_general | solution.py:16
  623.4 11.2 %all-reduce.17 = (f32[9]{0:T(128)S(1)}, f32[]{:T(128)}, f32[8,9]{1,0:T(8,128)S(1)}, f32[8]{0:T(128)S(1)}, f32[2048]{0:T(1024)S(1)}, /*index=5*/f32[8]{0:T(128)S(1)}) all-reduce(f32[9]{0:T(128)S(1)} %convolution_bitcast_fusion.24, f32[]{:T(128)} %get-tuple-element.729, ...), channel_id=1, replica_groups=mesh['prow'=8,'pcol'=4] {'pcol'}, use_global_device_ids=true, to_apply=%region_65.66 | all-reduce | flops 2146 | bytes 17168 | tf_op jit(solution)/shard_map/psum | solution.py:94
  638.7 4.7 scatter.200
  647.9 19.5 %fusion.331 = f32[1,4096]{1,0:T(1,128)S(1)} fusion(f32[2048,1]{0,1:T(1,128)S(1)} %bitcast.793, f32[2048,4096]{1,0:T(8,128)} %param.99), kind=kOutput, calls=%fused_computation.540 | convolution fusion | flops 100663296 | bytes 33579008 | tf_op jit(solution)/shard_map/dot_general | solution.py:16
  668.1 34.1 %all-reduce.8 = (f32[8]{0:T(128)S(1)}, f32[4096]{0:T(1024)S(1)}, f32[8]{0:T(128)S(1)}, f32[8]{0:T(128)S(1)}, f32[]{:T(128)}, /*index=5*/f32[8,8]{1,0:T(8,128)S(1)}) all-reduce(f32[8]{0:T(128)S(1)} %convolution_bitcast_fusion.20, f32[4096]{0:T(1024)S(1)} %bitcast.816, ...), channel_id=1, replica_groups=mesh['prow'=8,'pcol'=4] {'prow'}, use_global_device_ids=true, to_apply=%region_76.77 | all-reduce | flops 4185 | bytes 33480 | tf_op jit(solution)/shard_map/psum | solution.py:65
  710.1 30.7 %fusion.332 = f32[1,2048]{1,0:T(1,128)S(1)} fusion(f32[4096,1]{0,1:T(1,128)S(1)} %bitcast.766, f32[2048,4096]{1,0:T(8,128)} %param.99), kind=kOutput, calls=%fused_computation.541 | convolution fusion | flops 100663296 | bytes 33579008 | tf_op jit(solution)/shard_map/dot_general | solution.py:16
  741.1 11.2 %all-reduce.16 = (f32[9]{0:T(128)S(1)}, f32[]{:T(128)}, f32[8,9]{1,0:T(8,128)S(1)}, f32[8]{0:T(128)S(1)}, f32[2048]{0:T(1024)S(1)}, /*index=5*/f32[8]{0:T(128)S(1)}) all-reduce(f32[9]{0:T(128)S(1)} %convolution_bitcast_fusion.19, f32[]{:T(128)} %get-tuple-element.722, ...), channel_id=1, replica_groups=mesh['prow'=8,'pcol'=4] {'pcol'}, use_global_device_ids=true, to_apply=%region_79.80 | all-reduce | flops 2146 | bytes 17168 | tf_op jit(solution)/shard_map/psum | solution.py:94
  756.2 4.7 scatter.210
  765.4 19.5 %fusion.333 = f32[1,4096]{1,0:T(1,128)S(1)} fusion(f32[2048,1]{0,1:T(1,128)S(1)} %bitcast.797, f32[2048,4096]{1,0:T(8,128)} %param.99), kind=kOutput, calls=%fused_computation.542 | convolution fusion | flops 100663296 | bytes 33579008 | tf_op jit(solution)/shard_map/dot_general | solution.py:16
  785.5 34.1 %all-reduce.7 = (f32[8]{0:T(128)S(1)}, f32[4096]{0:T(1024)S(1)}, f32[8]{0:T(128)S(1)}, f32[8]{0:T(128)S(1)}, f32[]{:T(128)}, /*index=5*/f32[8,8]{1,0:T(8,128)S(1)}) all-reduce(f32[8]{0:T(128)S(1)} %convolution_bitcast_fusion.15, f32[4096]{0:T(1024)S(1)} %bitcast.817, ...), channel_id=1, replica_groups=mesh['prow'=8,'pcol'=4] {'prow'}, use_global_device_ids=true, to_apply=%region_90.91 | all-reduce | flops 4185 | bytes 33480 | tf_op jit(solution)/shard_map/psum | solution.py:65
  827.1 30.7 %fusion.334 = f32[1,2048]{1,0:T(1,128)S(1)} fusion(f32[4096,1]{0,1:T(1,128)S(1)} %bitcast.750, f32[2048,4096]{1,0:T(8,128)} %param.99), kind=kOutput, calls=%fused_computation.543 | convolution fusion | flops 100663296 | bytes 33579008 | tf_op jit(solution)/shard_map/dot_general | solution.py:16
  858.1 11.2 %all-reduce.15 = (f32[9]{0:T(128)S(1)}, f32[]{:T(128)}, f32[8,9]{1,0:T(8,128)S(1)}, f32[8]{0:T(128)S(1)}, f32[2048]{0:T(1024)S(1)}, /*index=5*/f32[8]{0:T(128)S(1)}) all-reduce(f32[9]{0:T(128)S(1)} %convolution_bitcast_fusion.14, f32[]{:T(128)} %get-tuple-element.715, ...), channel_id=1, replica_groups=mesh['prow'=8,'pcol'=4] {'pcol'}, use_global_device_ids=true, to_apply=%region_93.94 | all-reduce | flops 2146 | bytes 17168 | tf_op jit(solution)/shard_map/psum | solution.py:94
  872.9 4.7 scatter.220
  882.1 19.5 %fusion.335 = f32[1,4096]{1,0:T(1,128)S(1)} fusion(f32[2048,1]{0,1:T(1,128)S(1)} %bitcast.781, f32[2048,4096]{1,0:T(8,128)} %param.99), kind=kOutput, calls=%fused_computation.544 | convolution fusion | flops 100663296 | bytes 33579008 | tf_op jit(solution)/shard_map/dot_general | solution.py:16
  902.3 34.0 %all-reduce.6 = (f32[8]{0:T(128)S(1)}, f32[4096]{0:T(1024)S(1)}, f32[8]{0:T(128)S(1)}, f32[8]{0:T(128)S(1)}, f32[]{:T(128)}, /*index=5*/f32[8,8]{1,0:T(8,128)S(1)}) all-reduce(f32[8]{0:T(128)S(1)} %convolution_bitcast_fusion.10, f32[4096]{0:T(1024)S(1)} %bitcast.812, ...), channel_id=1, replica_groups=mesh['prow'=8,'pcol'=4] {'prow'}, use_global_device_ids=true, to_apply=%region_105.106 | all-reduce | flops 4185 | bytes 33480 | tf_op jit(solution)/shard_map/psum | solution.py:65
  943.6 30.7 %fusion.336 = f32[1,2048]{1,0:T(1,128)S(1)} fusion(f32[4096,1]{0,1:T(1,128)S(1)} %bitcast.770, f32[2048,4096]{1,0:T(8,128)} %param.99), kind=kOutput, calls=%fused_computation.545 | convolution fusion | flops 100663296 | bytes 33579008 | tf_op jit(solution)/shard_map/dot_general | solution.py:16
  974.6 11.1 %all-reduce.14 = (f32[9]{0:T(128)S(1)}, f32[]{:T(128)}, f32[8,9]{1,0:T(8,128)S(1)}, f32[8]{0:T(128)S(1)}, f32[2048]{0:T(1024)S(1)}, /*index=5*/f32[8]{0:T(128)S(1)}) all-reduce(f32[9]{0:T(128)S(1)} %convolution_bitcast_fusion.9, f32[]{:T(128)} %get-tuple-element.708, ...), channel_id=1, replica_groups=mesh['prow'=8,'pcol'=4] {'pcol'}, use_global_device_ids=true, to_apply=%region_106.107 | all-reduce | flops 2146 | bytes 17168 | tf_op jit(solution)/shard_map/psum | solution.py:94
  989.3 4.7 scatter.230
  997.8 32.9 %convolution_subtract_fusion = f32[2048,4096]{1,0:T(8,128)} fusion(f32[2048,4096]{1,0:T(8,128)} %param.99, f32[8,4096]{1,0:T(8,128)S(1)} %scatter.239, f32[8,4096]{1,0:T(8,128)S(1)} %scatter.235, f32[8,2048]{1,0:T(8,128)S(1)} %scatter.236, f32[8,2048]{1,0:T(8,128)S(1)} %copy.27), kind=kOutput, calls=%fused_computation | convolution fusion | flops 1619099648 | bytes 67502080 | tf_op jit(solution)/shard_map/dot_general | solution.py:135
  1030.6 2.3 select_select_fusion
  1032.9 5.8 scatter.240
  1039.7 1.8 fusion.2
  (309 shorter events, 93.4 us)
Async XLA Ops:
  7.2 42.8 %all-reduce.25.cloned.1.call-start = ((), (), s32[]{:S(2)}) async-start(), calls=%async_computation | async-start | bytes 2097152 | tf_op jit(solution)/shard_map/psum | solution.py:12
  9.5 114.8 %all-reduce.27.cloned.1.call-start = ((), (), s32[]{:S(2)}) async-start(), calls=%async_computation.1 | async-start | bytes 262144 | tf_op jit(solution)/shard_map/psum | solution.py:12
  882.1 114.7 %copy-start.1 = (f32[2048]{0:T(1024)S(1)}, f32[2048]{0:T(1024)}, u32[]{:S(2)}) copy-start(f32[2048]{0:T(1024)} %get-tuple-element.590) | copy-start | bytes 24580
  997.7 32.9 %copy-start.2 = (pred[2048]{0:T(1024)(128)(4,1)S(1)}, pred[2048]{0:T(1024)(128)(4,1)}, u32[]{:S(2)}) copy-start(pred[2048]{0:T(1024)(128)(4,1)} %fusion.145) | copy-start | bytes 6148
  997.8 41.9 %copy-start = (pred[9,4096]{1,0:T(8,128)(4,1)S(1)}, pred[9,4096]{1,0:T(8,128)(4,1)}, u32[]{:S(2)}) copy-start(pred[9,4096]{1,0:T(8,128)(4,1)} %iota_compare_fusion) | copy-start | bytes 110596
  997.8 41.9 %copy-start.3 = (pred[4096]{0:T(1024)(128)(4,1)S(1)}, pred[4096]{0:T(1024)(128)(4,1)}, u32[]{:S(2)}) copy-start(pred[4096]{0:T(1024)(128)(4,1)} %fusion.94) | copy-start | bytes 12292
  997.8 41.9 %copy-start.4 = (s32[8]{0:T(128)S(1)}, s32[8]{0:T(128)}, u32[]{:S(2)}) copy-start(s32[8]{0:T(128)} %iota_add_fusion.2) | copy-start | bytes 100
Sparse Core Ops, SparseCore 0:
  10.9 38.9 all-reduce.24
  53.3 71.0 all-reduce.26
where the time goes:
time: 1060 us; the launch traced here: 1050 us
  matrix products  483 us (46%)
  blocking collectives  369 us (35%)
  local copies, waits for them, and re-layouts  80.7 us (8%)
  between operations  56.4 us (5%)
  waiting for transfers between devices  38 us (4%)
  other arithmetic  21.1 us (2%)
    dot_general x134, matrix products, precise_dot(): return jnp.dot(left, right, precision=lax.Precision.HIGHEST)  447 us
    psum x8, blocking collectives, per_device(): lax.psum((precise_dot(masked, held_tile), precise_dot(v_rows, masked), pr...  280 us
    psum x8, blocking collectives, per_device(): lax.psum((precise_dot(held_tile, row_masked), precise_dot(y_cols, row_mas...  89.6 us
    psum x2, waiting for transfers between devices, from_root(): return lax.psum(jnp.where(mine, x, jnp.zeros_like(x)), axis)  38 us
    scatter x9, local copies, waits for them, and re-layouts, per_device(): v_rows = v_rows.at[i].set(v_new)  33.3 us
    dot_general x1, matrix products, per_device(): lax.dot_general(stack_left, stack_right, (((0,), (0,)), ((), ())), precis...  32.9 us
  transfers between devices with their start and end apart: 2, of which 2 were waited for; matrix products, arithmetic and copies ran while one was open for 4% of the time, Pallas kernels for 0%

commit v1 on v0

--- a/solution.py
+++ b/solution.py
@@ -9,7 +9,7 @@
 
 def from_root(x, axis, root):
     mine = lax.axis_index(axis) == root
-    return lax.psum(jnp.where(mine, x, jnp.zeros_like(x)), axis)
+    return jnp.sum(jax.lax.all_gather(jnp.where(mine, x, jnp.zeros_like(x)), axis_name=axis), 0)
 
 
 def precise_dot(left, right):

time: 1060 us -> 1010 us (0.953)
  waiting for transfers between devices: 38 us -> 0.02 us
    psum x2 -> x0, waiting for transfers between devices: 38 us -> none  [from_root(): return lax.psum(jnp.where(mine, x, jnp.zeros_like(x)), axis)]
  transfers between devices with their start and end apart: 2 -> 1, of which waited for: 2 -> 0; matrix products, arithmetic and copies ran while one was open for 4% -> 3% of each run, Pallas kernels for 0% -> 0%
where the time goes in v1:
time: 1010 us; the launch traced here: 1000 us
  matrix products  484 us (48%)
  blocking collectives  376 us (37%)
  local copies, waits for them, and re-layouts  70.6 us (7%)
  between operations  54.2 us (5%)
  other arithmetic  19.4 us (2%)
    dot_general x134, matrix products, precise_dot(): return jnp.dot(left, right, precision=lax.Precision.HIGHEST)  447 us
    psum x8, blocking collectives, per_device(): lax.psum((precise_dot(masked, held_tile), precise_dot(v_rows, masked), pr...  277 us
    psum x8, blocking collectives, per_device(): lax.psum((precise_dot(held_tile, row_masked), precise_dot(y_cols, row_mas...  89.7 us
    scatter x9, local copies, waits for them, and re-layouts, per_device(): v_rows = v_rows.at[i].set(v_new)  33.3 us
    dot_general x1, matrix products, per_device(): lax.dot_general(stack_left, stack_right, (((0,), (0,)), ((), ())), precis...  32.8 us
  transfers between devices with their start and end apart: 1, of which 0 were waited for; matrix products, arithmetic and copies ran while one was open for 3% of the time, Pallas kernels for 0%

profile of v1, /device:TPU:0, one launch (start us, length us, event | category | flops | bytes accessed | tf_op | source)
XLA Modules:
  0.0 1003.3 jit_solution(11703961645701190652)
XLA Ops:
  7.2 1.6 slice_select_fusion
  8.8 1.3 slice.972
  10.7 8.7 all-gather.2
  20.6 19.6 %fusion.322 = f32[1,4096]{1,0:T(1,128)S(1)} fusion(f32[2048,1]{0,1:T(1,128)S(1)} %bitcast.821, f32[2048,4096]{1,0:T(8,128)} %param.99), kind=kOutput, calls=%fused_computation.523 | convolution fusion | flops 100663296 | bytes 33579008 | tf_op jit(solution)/shard_map/dot_general | solution.py:16
  40.8 38.8 %all-reduce.13 = (f32[8]{0:T(128)S(1)}, f32[4096]{0:T(1024)S(1)}, f32[8]{0:T(128)S(1)}, f32[]{:T(128)}, f32[8,8]{1,0:T(8,128)S(1)}) all-reduce(f32[8]{0:T(128)S(1)} %convolution_bitcast_fusion.45, f32[4096]{0:T(1024)S(1)} %bitcast.831, f32[8]{0:T(128)S(1)} %convolution_bitcast_fusion.46, ...), channel_id=1, replica_groups=mesh['prow'=8,'pcol'=4] {'prow'}, use_global_device_ids=true, to_apply=%region_5.6 | all-reduce | flops 4177 | bytes 33416 | tf_op jit(solution)/shard_map/psum | solution.py:65
  85.1 1.3 bitcast_reduce_fusion
  88.0 30.7 %fusion.323 = f32[1,2048]{1,0:T(1,128)S(1)} fusion(f32[4096,1]{0,1:T(1,128)S(1)} %bitcast.815, f32[2048,4096]{1,0:T(8,128)} %param.99), kind=kOutput, calls=%fused_computation.524 | convolution fusion | flops 100663296 | bytes 33579008 | tf_op jit(solution)/shard_map/dot_general | solution.py:16
  119.1 11.7 %all-reduce.21 = (f32[9]{0:T(128)S(1)}, f32[]{:T(128)}, f32[8,9]{1,0:T(8,128)S(1)}, f32[8]{0:T(128)S(1)}, f32[2048]{0:T(1024)S(1)}, /*index=5*/f32[8]{0:T(128)S(1)}) all-reduce(f32[9]{0:T(128)S(1)} %convolution_bitcast_fusion.44, f32[]{:T(128)} %get-tuple-element.748, ...), channel_id=1, replica_groups=mesh['prow'=8,'pcol'=4] {'pcol'}, use_global_device_ids=true, to_apply=%region_9.10 | all-reduce | flops 2146 | bytes 17168 | tf_op jit(solution)/shard_map/psum | solution.py:94
  137.8 19.5 %fusion.324 = f32[1,4096]{1,0:T(1,128)S(1)} fusion(f32[2048,1]{0,1:T(1,128)S(1)} %bitcast.818, f32[2048,4096]{1,0:T(8,128)} %param.99), kind=kOutput, calls=%fused_computation.525 | convolution fusion | flops 100663296 | bytes 33579008 | tf_op jit(solution)/shard_map/dot_general | solution.py:16
  157.9 34.0 %all-reduce.12 = (f32[8]{0:T(128)S(1)}, f32[4096]{0:T(1024)S(1)}, f32[8]{0:T(128)S(1)}, f32[8]{0:T(128)S(1)}, f32[]{:T(128)}, /*index=5*/f32[8,8]{1,0:T(8,128)S(1)}) all-reduce(f32[8]{0:T(128)S(1)} %convolution_bitcast_fusion.40, f32[4096]{0:T(1024)S(1)} %bitcast.826, ...), channel_id=1, replica_groups=mesh['prow'=8,'pcol'=4] {'prow'}, use_global_device_ids=true, to_apply=%region_20.21 | all-reduce | flops 4185 | bytes 33480 | tf_op jit(solution)/shard_map/psum | solution.py:65
  198.5 30.7 %fusion.325 = f32[1,2048]{1,0:T(1,128)S(1)} fusion(f32[4096,1]{0,1:T(1,128)S(1)} %bitcast.787, f32[2048,4096]{1,0:T(8,128)} %param.99), kind=kOutput, calls=%fused_computation.526 | convolution fusion | flops 100663296 | bytes 33579008 | tf_op jit(solution)/shard_map/dot_general | solution.py:16
  229.6 11.1 %all-reduce.20 = (f32[9]{0:T(128)S(1)}, f32[]{:T(128)}, f32[8,9]{1,0:T(8,128)S(1)}, f32[8]{0:T(128)S(1)}, f32[2048]{0:T(1024)S(1)}, /*index=5*/f32[8]{0:T(128)S(1)}) all-reduce(f32[9]{0:T(128)S(1)} %convolution_bitcast_fusion.39, f32[]{:T(128)} %get-tuple-element.741, ...), channel_id=1, replica_groups=mesh['prow'=8,'pcol'=4] {'pcol'}, use_global_device_ids=true, to_apply=%region_23.24 | all-reduce | flops 2146 | bytes 17168 | tf_op jit(solution)/shard_map/psum | solution.py:94
  244.6 4.7 scatter.170
  250.2 0.9 fusion.279
  253.7 19.5 %fusion.326 = f32[1,4096]{1,0:T(1,128)S(1)} fusion(f32[2048,1]{0,1:T(1,128)S(1)} %bitcast.790, f32[2048,4096]{1,0:T(8,128)} %param.99), kind=kOutput, calls=%fused_computation.527 | convolution fusion | flops 100663296 | bytes 33579008 | tf_op jit(solution)/shard_map/dot_general | solution.py:16
  273.9 34.0 %all-reduce.11 = (f32[8]{0:T(128)S(1)}, f32[4096]{0:T(1024)S(1)}, f32[8]{0:T(128)S(1)}, f32[8]{0:T(128)S(1)}, f32[]{:T(128)}, /*index=5*/f32[8,8]{1,0:T(8,128)S(1)}) all-reduce(f32[8]{0:T(128)S(1)} %convolution_bitcast_fusion.35, f32[4096]{0:T(1024)S(1)} %bitcast.824, ...), channel_id=1, replica_groups=mesh['prow'=8,'pcol'=4] {'prow'}, use_global_device_ids=true, to_apply=%region_34.35 | all-reduce | flops 4185 | bytes 33480 | tf_op jit(solution)/shard_map/psum | solution.py:65
  315.3 30.7 %fusion.327 = f32[1,2048]{1,0:T(1,128)S(1)} fusion(f32[4096,1]{0,1:T(1,128)S(1)} %bitcast.767, f32[2048,4096]{1,0:T(8,128)} %param.99), kind=kOutput, calls=%fused_computation.528 | convolution fusion | flops 100663296 | bytes 33579008 | tf_op jit(solution)/shard_map/dot_general | solution.py:16
  346.3 11.1 %all-reduce.19 = (f32[9]{0:T(128)S(1)}, f32[]{:T(128)}, f32[8,9]{1,0:T(8,128)S(1)}, f32[8]{0:T(128)S(1)}, f32[2048]{0:T(1024)S(1)}, /*index=5*/f32[8]{0:T(128)S(1)}) all-reduce(f32[9]{0:T(128)S(1)} %convolution_bitcast_fusion.34, f32[]{:T(128)} %get-tuple-element.734, ...), channel_id=1, replica_groups=mesh['prow'=8,'pcol'=4] {'pcol'}, use_global_device_ids=true, to_apply=%region_37.38 | all-reduce | flops 2146 | bytes 17168 | tf_op jit(solution)/shard_map/psum | solution.py:94
  361.1 4.7 scatter.180
  370.2 19.5 %fusion.328 = f32[1,4096]{1,0:T(1,128)S(1)} fusion(f32[2048,1]{0,1:T(1,128)S(1)} %bitcast.798, f32[2048,4096]{1,0:T(8,128)} %param.99), kind=kOutput, calls=%fused_computation.529 | convolution fusion | flops 100663296 | bytes 33579008 | tf_op jit(solution)/shard_map/dot_general | solution.py:16
  390.4 34.0 %all-reduce.10 = (f32[8]{0:T(128)S(1)}, f32[4096]{0:T(1024)S(1)}, f32[8]{0:T(128)S(1)}, f32[8]{0:T(128)S(1)}, f32[]{:T(128)}, /*index=5*/f32[8,8]{1,0:T(8,128)S(1)}) all-reduce(f32[8]{0:T(128)S(1)} %convolution_bitcast_fusion.30, f32[4096]{0:T(1024)S(1)} %bitcast.827, ...), channel_id=1, replica_groups=mesh['prow'=8,'pcol'=4] {'prow'}, use_global_device_ids=true, to_apply=%region_48.49 | all-reduce | flops 4185 | bytes 33480 | tf_op jit(solution)/shard_map/psum | solution.py:65
  431.6 30.7 %fusion.329 = f32[1,2048]{1,0:T(1,128)S(1)} fusion(f32[4096,1]{0,1:T(1,128)S(1)} %bitcast.771, f32[2048,4096]{1,0:T(8,128)} %param.99), kind=kOutput, calls=%fused_computation.530 | convolution fusion | flops 100663296 | bytes 33579008 | tf_op jit(solution)/shard_map/dot_general | solution.py:16
  462.6 11.1 %all-reduce.18 = (f32[9]{0:T(128)S(1)}, f32[]{:T(128)}, f32[8,9]{1,0:T(8,128)S(1)}, f32[8]{0:T(128)S(1)}, f32[2048]{0:T(1024)S(1)}, /*index=5*/f32[8]{0:T(128)S(1)}) all-reduce(f32[9]{0:T(128)S(1)} %convolution_bitcast_fusion.29, f32[]{:T(128)} %get-tuple-element.727, ...), channel_id=1, replica_groups=mesh['prow'=8,'pcol'=4] {'pcol'}, use_global_device_ids=true, to_apply=%region_51.52 | all-reduce | flops 2146 | bytes 17168 | tf_op jit(solution)/shard_map/psum | solution.py:94
  477.6 4.7 scatter.190
  487.0 19.5 %fusion.330 = f32[1,4096]{1,0:T(1,128)S(1)} fusion(f32[2048,1]{0,1:T(1,128)S(1)} %bitcast.802, f32[2048,4096]{1,0:T(8,128)} %param.99), kind=kOutput, calls=%fused_computation.531 | convolution fusion | flops 100663296 | bytes 33579008 | tf_op jit(solution)/shard_map/dot_general | solution.py:16
  507.2 34.0 %all-reduce.9 = (f32[8]{0:T(128)S(1)}, f32[4096]{0:T(1024)S(1)}, f32[8]{0:T(128)S(1)}, f32[8]{0:T(128)S(1)}, f32[]{:T(128)}, /*index=5*/f32[8,8]{1,0:T(8,128)S(1)}) all-reduce(f32[8]{0:T(128)S(1)} %convolution_bitcast_fusion.25, f32[4096]{0:T(1024)S(1)} %bitcast.828, ...), channel_id=1, replica_groups=mesh['prow'=8,'pcol'=4] {'prow'}, use_global_device_ids=true, to_apply=%region_62.63 | all-reduce | flops 4185 | bytes 33480 | tf_op jit(solution)/shard_map/psum | solution.py:65
  548.6 30.7 %fusion.331 = f32[1,2048]{1,0:T(1,128)S(1)} fusion(f32[4096,1]{0,1:T(1,128)S(1)} %bitcast.775, f32[2048,4096]{1,0:T(8,128)} %param.99), kind=kOutput, calls=%fused_computation.532 | convolution fusion | flops 100663296 | bytes 33579008 | tf_op jit(solution)/shard_map/dot_general | solution.py:16
  579.6 11.1 %all-reduce.17 = (f32[9]{0:T(128)S(1)}, f32[]{:T(128)}, f32[8,9]{1,0:T(8,128)S(1)}, f32[8]{0:T(128)S(1)}, f32[2048]{0:T(1024)S(1)}, /*index=5*/f32[8]{0:T(128)S(1)}) all-reduce(f32[9]{0:T(128)S(1)} %convolution_bitcast_fusion.24, f32[]{:T(128)} %get-tuple-element.720, ...), channel_id=1, replica_groups=mesh['prow'=8,'pcol'=4] {'pcol'}, use_global_device_ids=true, to_apply=%region_65.66 | all-reduce | flops 2146 | bytes 17168 | tf_op jit(solution)/shard_map/psum | solution.py:94
  594.3 4.7 scatter.200
  603.5 19.5 %fusion.332 = f32[1,4096]{1,0:T(1,128)S(1)} fusion(f32[2048,1]{0,1:T(1,128)S(1)} %bitcast.806, f32[2048,4096]{1,0:T(8,128)} %param.99), kind=kOutput, calls=%fused_computation.533 | convolution fusion | flops 100663296 | bytes 33579008 | tf_op jit(solution)/shard_map/dot_general | solution.py:16
  623.7 34.0 %all-reduce.8 = (f32[8]{0:T(128)S(1)}, f32[4096]{0:T(1024)S(1)}, f32[8]{0:T(128)S(1)}, f32[8]{0:T(128)S(1)}, f32[]{:T(128)}, /*index=5*/f32[8,8]{1,0:T(8,128)S(1)}) all-reduce(f32[8]{0:T(128)S(1)} %convolution_bitcast_fusion.20, f32[4096]{0:T(1024)S(1)} %bitcast.829, ...), channel_id=1, replica_groups=mesh['prow'=8,'pcol'=4] {'prow'}, use_global_device_ids=true, to_apply=%region_76.77 | all-reduce | flops 4185 | bytes 33480 | tf_op jit(solution)/shard_map/psum | solution.py:65
  664.9 30.7 %fusion.333 = f32[1,2048]{1,0:T(1,128)S(1)} fusion(f32[4096,1]{0,1:T(1,128)S(1)} %bitcast.779, f32[2048,4096]{1,0:T(8,128)} %param.99), kind=kOutput, calls=%fused_computation.534 | convolution fusion | flops 100663296 | bytes 33579008 | tf_op jit(solution)/shard_map/dot_general | solution.py:16
  695.9 11.1 %all-reduce.16 = (f32[9]{0:T(128)S(1)}, f32[]{:T(128)}, f32[8,9]{1,0:T(8,128)S(1)}, f32[8]{0:T(128)S(1)}, f32[2048]{0:T(1024)S(1)}, /*index=5*/f32[8]{0:T(128)S(1)}) all-reduce(f32[9]{0:T(128)S(1)} %convolution_bitcast_fusion.19, f32[]{:T(128)} %get-tuple-element.713, ...), channel_id=1, replica_groups=mesh['prow'=8,'pcol'=4] {'pcol'}, use_global_device_ids=true, to_apply=%region_79.80 | all-reduce | flops 2146 | bytes 17168 | tf_op jit(solution)/shard_map/psum | solution.py:94
  710.6 4.7 scatter.210
  720.0 19.5 %fusion.334 = f32[1,4096]{1,0:T(1,128)S(1)} fusion(f32[2048,1]{0,1:T(1,128)S(1)} %bitcast.810, f32[2048,4096]{1,0:T(8,128)} %param.99), kind=kOutput, calls=%fused_computation.535 | convolution fusion | flops 100663296 | bytes 33579008 | tf_op jit(solution)/shard_map/dot_general | solution.py:16
  740.1 34.0 %all-reduce.7 = (f32[8]{0:T(128)S(1)}, f32[4096]{0:T(1024)S(1)}, f32[8]{0:T(128)S(1)}, f32[8]{0:T(128)S(1)}, f32[]{:T(128)}, /*index=5*/f32[8,8]{1,0:T(8,128)S(1)}) all-reduce(f32[8]{0:T(128)S(1)} %convolution_bitcast_fusion.15, f32[4096]{0:T(1024)S(1)} %bitcast.830, ...), channel_id=1, replica_groups=mesh['prow'=8,'pcol'=4] {'prow'}, use_global_device_ids=true, to_apply=%region_90.91 | all-reduce | flops 4185 | bytes 33480 | tf_op jit(solution)/shard_map/psum | solution.py:65
  781.2 30.7 %fusion.335 = f32[1,2048]{1,0:T(1,128)S(1)} fusion(f32[4096,1]{0,1:T(1,128)S(1)} %bitcast.763, f32[2048,4096]{1,0:T(8,128)} %param.99), kind=kOutput, calls=%fused_computation.536 | convolution fusion | flops 100663296 | bytes 33579008 | tf_op jit(solution)/shard_map/dot_general | solution.py:16
  812.2 11.1 %all-reduce.15 = (f32[9]{0:T(128)S(1)}, f32[]{:T(128)}, f32[8,9]{1,0:T(8,128)S(1)}, f32[8]{0:T(128)S(1)}, f32[2048]{0:T(1024)S(1)}, /*index=5*/f32[8]{0:T(128)S(1)}) all-reduce(f32[9]{0:T(128)S(1)} %convolution_bitcast_fusion.14, f32[]{:T(128)} %get-tuple-element.706, ...), channel_id=1, replica_groups=mesh['prow'=8,'pcol'=4] {'pcol'}, use_global_device_ids=true, to_apply=%region_93.94 | all-reduce | flops 2146 | bytes 17168 | tf_op jit(solution)/shard_map/psum | solution.py:94
  827.2 4.7 scatter.220
  836.3 19.5 %fusion.336 = f32[1,4096]{1,0:T(1,128)S(1)} fusion(f32[2048,1]{0,1:T(1,128)S(1)} %bitcast.794, f32[2048,4096]{1,0:T(8,128)} %param.99), kind=kOutput, calls=%fused_computation.537 | convolution fusion | flops 100663296 | bytes 33579008 | tf_op jit(solution)/shard_map/dot_general | solution.py:16
  856.5 34.0 %all-reduce.6 = (f32[8]{0:T(128)S(1)}, f32[4096]{0:T(1024)S(1)}, f32[8]{0:T(128)S(1)}, f32[8]{0:T(128)S(1)}, f32[]{:T(128)}, /*index=5*/f32[8,8]{1,0:T(8,128)S(1)}) all-reduce(f32[8]{0:T(128)S(1)} %convolution_bitcast_fusion.10, f32[4096]{0:T(1024)S(1)} %bitcast.825, ...), channel_id=1, replica_groups=mesh['prow'=8,'pcol'=4] {'prow'}, use_global_device_ids=true, to_apply=%region_105.106 | all-reduce | flops 4185 | bytes 33480 | tf_op jit(solution)/shard_map/psum | solution.py:65
  897.9 30.7 %fusion.337 = f32[1,2048]{1,0:T(1,128)S(1)} fusion(f32[4096,1]{0,1:T(1,128)S(1)} %bitcast.783, f32[2048,4096]{1,0:T(8,128)} %param.99), kind=kOutput, calls=%fused_computation.538 | convolution fusion | flops 100663296 | bytes 33579008 | tf_op jit(solution)/shard_map/dot_general | solution.py:16
  929.0 11.1 %all-reduce.14 = (f32[9]{0:T(128)S(1)}, f32[]{:T(128)}, f32[8,9]{1,0:T(8,128)S(1)}, f32[8]{0:T(128)S(1)}, f32[2048]{0:T(1024)S(1)}, /*index=5*/f32[8]{0:T(128)S(1)}) all-reduce(f32[9]{0:T(128)S(1)} %convolution_bitcast_fusion.9, f32[]{:T(128)} %get-tuple-element.699, ...), channel_id=1, replica_groups=mesh['prow'=8,'pcol'=4] {'pcol'}, use_global_device_ids=true, to_apply=%region_106.107 | all-reduce | flops 2146 | bytes 17168 | tf_op jit(solution)/shard_map/psum | solution.py:94
  943.9 4.7 scatter.230
  952.4 32.8 %convolution_subtract_fusion = f32[2048,4096]{1,0:T(8,128)} fusion(f32[2048,4096]{1,0:T(8,128)} %param.99, f32[8,4096]{1,0:T(8,128)S(1)} %scatter.239, f32[8,4096]{1,0:T(8,128)S(1)} %scatter.235, f32[8,2048]{1,0:T(8,128)S(1)} %scatter.236, f32[8,2048]{1,0:T(8,128)S(1)} %copy.40), kind=kOutput, calls=%fused_computation | convolution fusion | flops 1619099648 | bytes 67502080 | tf_op jit(solution)/shard_map/dot_general | solution.py:135
  985.3 2.2 select_select_fusion
  987.5 5.8 scatter.240
  994.3 1.8 fusion.2
  (311 shorter events, 90.8 us)
Async XLA Ops:
  7.2 77.9 %all-gather.5.cloned.1.call-start = ((), (), s32[]{:S(2)}) async-start(), calls=%async_computation | async-start | bytes 1179648 | tf_op jit(solution)/shard_map/all_gather | solution.py:12
  836.3 115.2 %copy-start.1 = (f32[1,2048]{1,0:T(1,128)S(1)}, f32[1,2048]{1,0:T(1,128)}, u32[]{:S(2)}) copy-start(f32[1,2048]{1,0:T(1,128)} %get-tuple-element.753) | copy-start | bytes 24580
  952.4 32.9 %copy-start.2 = (pred[2048]{0:T(1024)(128)(4,1)S(1)}, pred[2048]{0:T(1024)(128)(4,1)}, u32[]{:S(2)}) copy-start(pred[2048]{0:T(1024)(128)(4,1)} %fusion.145) | copy-start | bytes 6148
  952.4 41.8 %copy-start = (pred[9,4096]{1,0:T(8,128)(4,1)S(1)}, pred[9,4096]{1,0:T(8,128)(4,1)}, u32[]{:S(2)}) copy-start(pred[9,4096]{1,0:T(8,128)(4,1)} %iota_compare_fusion) | copy-start | bytes 110596
  952.4 41.8 %copy-start.3 = (pred[4096]{0:T(1024)(128)(4,1)S(1)}, pred[4096]{0:T(1024)(128)(4,1)}, u32[]{:S(2)}) copy-start(pred[4096]{0:T(1024)(128)(4,1)} %fusion.94) | copy-start | bytes 12292
  952.4 41.8 %copy-start.4 = (s32[8]{0:T(128)S(1)}, s32[8]{0:T(128)}, u32[]{:S(2)}) copy-start(s32[8]{0:T(128)} %iota_add_fusion.2) | copy-start | bytes 100
Sparse Core Ops, SparseCore 0:
  10.7 43.0 all-gather.4
